TPU v7x, 512 devices: a whole 4x8x8 slice. The times are simulated.
512 devices in a mesh: gy: 32 (over z, y_lo), gz: 16 (over x, y_hi, core).
Axes of the slice: x: 4, y: 8 (y_hi: 2, y_lo: 4; y = y_hi * 4 + y_lo), z: 8, core: 2. Of those that a mesh axis runs over, the one named last changes fastest.
Arguments:
- scalar: float32 [64, 768, 768], P('gz', 'gy'), may hold values from -6 to 6
- velocity: float32 [3, 64, 256, 256], P(None, None, 'gy', 'gz'), may hold values from -0.9 to 0.9
Outputs:
- remeshed: float32 [64, 768, 768], P('gz', 'gy')
All inputs are finite; a program needn't handle non-finite values.
Results may differ from a plain program's by a relative error of at most 0.0003.
Values sent between devices are 32-bit elements; how exact they have to be, the bound alone decides.
A program may use at most 64 MiB of HBM per device.

v0:
```python
import jax
import jax.numpy as jnp
from jax import lax
from jax.sharding import PartitionSpec as P


def padded_2(value, sides, width):
    for axis, dim in sides:
        peers, length = (lax.axis_size(axis), value.shape[dim])
        up = [(i, (i + 1) % peers) for i in range(peers - 1)]
        down = [(j, i) for i, j in up]
        last = lax.slice_in_dim(value, length - width, length, axis=dim)
        initial = lax.slice_in_dim(value, 0, width, axis=dim)
        before = lax.ppermute(last, axis, up)
        after = lax.ppermute(initial, axis, down)
        value = jnp.concatenate([before, value, after], axis=dim)
    return value


def passed_along(block, axis, distance):
    devices = range(lax.axis_size(axis))
    route = [((i - distance) % len(devices), i) for i in devices]
    return lax.ppermute(block, axis, route)


def alternate(current, following, along):
    pieces = [current * (1.0 - phase / 3.0) + following * (phase / 3.0) for phase in range(3)]
    stacked = jnp.stack(pieces, axis=along + 1)
    new_shape = list(current.shape)
    new_shape[along] = new_shape[along] * 3
    return stacked.reshape(new_shape)


def polynomial(factors, value):
    result = jnp.zeros_like(value)
    for factor in reversed(factors):
        result = result * value + factor
    return result


def kernel_weight(offset):
    size = jnp.abs(offset)
    inner = polynomial([1.0, 0.0, -5.0 / 4.0, -35.0 / 12.0, 21.0 / 4.0, -25.0 / 12.0], size)
    middle = polynomial(
        [-4.0, 75.0 / 4.0, -245.0 / 8.0, 545.0 / 24.0, -63.0 / 8.0, 25.0 / 24.0], size
    )
    outer = polynomial(
        [18.0, -153.0 / 4.0, 255.0 / 8.0, -313.0 / 24.0, 21.0 / 8.0, -5.0 / 24.0], size
    )
    return jnp.where(
        size < 1.0, inner, jnp.where(size < 2.0, middle, jnp.where(size < 3.0, outer, 0.0))
    )


def displacement(speed, before, after):
    half_step = 0.5 * speed
    return jnp.where(
        half_step >= 0.0,
        (1.0 - half_step) * speed + half_step * after,
        (1.0 + half_step) * speed - half_step * before,
    )


def sweep_periodic(field, speed, along):
    moved = displacement(speed, jnp.roll(speed, 1, along), jnp.roll(speed, -1, along))
    result = jnp.zeros_like(field)
    for offset in range(-3, 4):
        result = result + jnp.roll(field * kernel_weight(offset - moved), offset, along)
    return result


def sweep_open(field, speed, padded):
    padded = padded_2(speed, (("gz", 0),), 1)
    moved = displacement(speed, padded[:-2], padded[2:])
    count = field.shape[0]
    total = jnp.zeros((count + 6,) + field.shape[1:], jnp.float32)
    for offset in range(-3, 4):
        total = total.at[3 + offset : 3 + offset + count].add(field * kernel_weight(offset - moved))
    ghosts = jnp.concatenate([total[:3], total[count + 3 :]], axis=0)
    received = padded_2(ghosts, (("gz", 0),), 3)
    result = total[3 : count + 3]
    result = result.at[:3].add(received[:3])
    result = result.at[count - 3 :].add(received[9:])
    return result


def local(scalar, velocity):
    coarse = lax.all_to_all(velocity, "gz", split_axis=1, concat_axis=3, tiled=True)
    rows_part = coarse[:1]
    next_row = passed_along(rows_part[:, :, :1, :], "gy", -1)
    y_fine = alternate(rows_part, jnp.concatenate([rows_part[:, :, 1:, :], next_row], axis=2), 2)
    fine_vel = alternate(y_fine, jnp.roll(y_fine, -1, 3), 3)
    field = sweep_periodic(scalar, fine_vel[0], 2)
    turned = jnp.swapaxes(field, 1, 2)
    padded_z = None
    sending = coarse[1:]
    field = lax.all_to_all(turned, "gy", split_axis=1, concat_axis=2, tiled=True)
    coarse_rows = jnp.swapaxes(sending, 2, 3)
    coarse_turned = lax.all_to_all(coarse_rows, "gy", split_axis=2, concat_axis=3, tiled=True)
    y_refined = alternate(coarse_turned, jnp.roll(coarse_turned, -1, 3), 3)
    next_col = passed_along(y_refined[:, :, :1, :], "gy", -1)
    pencil_vel = alternate(
        y_refined, jnp.concatenate([y_refined[:, :, 1:, :], next_col], axis=2), 2
    )
    speed_y = pencil_vel[0]
    speed_z = pencil_vel[1]
    field = sweep_periodic(field, speed_y, 2)
    return sweep_open(field, speed_z, padded_z)


def solution(mesh):
    in_specs = (P("gz", "gy", None), P(None, None, "gy", "gz"))
    out_specs = P("gz", "gy", None)
    return jax.shard_map(local, mesh=mesh, in_specs=in_specs, out_specs=out_specs, check_vma=False)
```

profile of v0, /device:TPU:1, one launch (start us, length us, event | category | flops | bytes accessed | tf_op | source)
XLA Modules:
  0.0 137.3 jit_solution(2114219624516840462)
XLA Ops:
  0.0 1.2 copy.400
  1.6 20.6 %all_to_all.54 = f32[16,1,1536]{2,1,0:T(1,128)S(1)} all-to-all(f32[16,1,1536]{2,1,0:T(1,128)S(1)} %reshape.847), channel_id=1, replica_groups=mesh['gy'=32,'gz'=16] {'gz'}, dimensions={0} | all-to-all | bytes 196608 | tf_op jit(solution)/shard_map/all_to_all | solution.py:88
  22.7 0.8 reduce.18
  24.3 11.1 %collective-permute-start = (f32[1,4,1,256]{3,2,1,0:T(1,128)S(1)}, f32[1,4,1,256]{3,2,1,0:T(1,128)S(1)}, u32[]{:S(2)}, u32[]{:S(2)}) collective-permute-start(f32[1,4,1,256]{3,2,1,0:T(1,128)S(1)} %slice.470), channel_id=1, source_target_pairs={{16,0},{32,16},{48,32},{64,48},{80,64},{96,80},{112,96},{128,112},... | collective-permute-start | bytes 12296 | tf_op jit(solution)/shard_map/ppermute | solution.py:23
  36.6 1.8 %reshape.851 = f32[32,1,512]{2,1,0:T(1,128)} reshape(f32[256,2,4,8]{3,2,1,0:T(4,128)S(1)} %bitcast.82) | data formatting | bytes 131072
  38.4 3.9 %all-to-all-start.2 = ((f32[32,1,512]{2,1,0:T(1,128)}), f32[32,1,512]{2,1,0:T(1,128)S(1)}, u32[]{:S(2)}, u32[]{:S(2)}) async-start(f32[32,1,512]{2,1,0:T(1,128)} %reshape.851), calls=%async_computation.2 | async-start | bytes 131072 | tf_op jit(solution)/shard_map/all_to_all | solution.py:99
  42.9 0.8 copy.409
  45.1 2.0 %fusion.22 = (f32[4,24,768]{2,1,0:T(8,128)S(1)}, f32[4,24,768]{2,1,0:T(8,128)S(1)}, f32[4,24,768]{2,1,0:T(8,128)S(1)}, f32[4,24,768]{2,1,0:T(8,128)S(1)}, f32[4,24,768]{2,1,0:T(8,128)S(1)}) fusion(f32[4,24,768]{2,1,0:T(8,128)S(1)} %copy-done, f32[4,24,768]{2,1,0:T(8,128)S(1)} %get-tuple-element.121), kind=kLoop, calls=%fused_computation.47 | loop fusion | flops 15482880 | bytes 2064384 | tf_op jit(solution)/shard_map/mul | solution.py:68
  49.1 2.8 %reshape.849 = f32[32,1,2304]{2,1,0:T(1,128)} reshape(f32[768,4,24]{2,1,0:T(4,128)S(1)} %bitcast.76) | data formatting | bytes 589824
  51.9 9.7 %all-to-all-start.1 = ((f32[32,1,2304]{2,1,0:T(1,128)}), f32[32,1,2304]{2,1,0:T(1,128)S(1)}, u32[]{:S(2)}, u32[]{:S(2)}) async-start(f32[32,1,2304]{2,1,0:T(1,128)} %reshape.849), calls=%async_computation.1 | async-start | bytes 589824 | tf_op jit(solution)/shard_map/all_to_all | solution.py:97
  62.4 1.2 reshape.852
  66.2 2.6 %copy.426 = f32[2,4,8,256,3]{2,1,4,3,0:T(4,128)S(1)} copy(f32[2,4,8,256,3]{3,2,1,0,4:T(8,128)} %pad_maximum_fusion.4) | data formatting | bytes 393216 | tf_op jit(solution)/shard_map/stack | solution.py:28
  68.8 1.2 copy.428
  70.0 7.0 %collective-permute-start.1 = (f32[2,4,1,768]{3,1,2,0:T(4,128)S(1)}, f32[2,4,1,768]{3,1,2,0:T(4,128)S(1)}, u32[]{:S(2)}, u32[]{:S(2)}) collective-permute-start(f32[2,4,1,768]{3,1,2,0:T(4,128)S(1)} %copy.428), channel_id=1, source_target_pairs={{16,0},{32,16},{48,32},{64,48},{80,64},{96,80},{112,96},{128,112},... | collective-permute-start | bytes 73736 | tf_op jit(solution)/shard_map/ppermute | solution.py:23
  77.0 3.3 %slice_bitcast_fusion = f32[2,4,7,1,768]{2,1,4,0,3:T(4,128)} fusion(f32[2,4,8,768]{2,1,3,0:T(4,128)S(1)} %bitcast.71), kind=kLoop, calls=%fused_computation | loop fusion | bytes 344064 | tf_op jit(solution)/shard_map/concatenate | solution.py:103
  80.3 3.8 %copy.429 = f32[2,4,7,1,768]{4,2,3,1,0:T(8,128)} copy(f32[2,4,7,1,768]{2,1,4,0,3:T(4,128)} %slice_bitcast_fusion) | data formatting | bytes 344064 | tf_op jit(solution)/shard_map/concatenate | solution.py:103
  84.1 2.0 %copy.431 = f32[2,4,8,1,768]{4,2,3,1,0:T(8,128)} copy(f32[2,4,8,1,768]{2,1,4,0,3:T(4,128)S(1)} %bitcast.72) | data formatting | bytes 393216 | tf_op jit(solution)/shard_map/reshape | solution.py:31
  86.1 1.1 multiply_add_fusion.24
  87.6 3.9 %collective-permute-start.2 = (f32[1,24,768]{2,0,1:T(1,128)S(1)}, f32[1,24,768]{2,0,1:T(1,128)S(1)}, u32[]{:S(2)}, u32[]{:S(2)}) collective-permute-start(f32[1,24,768]{2,0,1:T(1,128)S(1)} %bitcast.98), channel_id=1, source_target_pairs={{1,0},{2,1},{3,2},{4,3},{5,4},{6,5},{7,6},{8,7},{9,8},{10,9},{11,1... | collective-permute-start | bytes 221192 | tf_op jit(solution)/shard_map/ppermute | solution.py:15
  91.6 5.6 %collective-permute-start.3 = (f32[1,24,768]{2,0,1:T(1,128)S(1)}, f32[1,24,768]{2,0,1:T(1,128)S(1)}, u32[]{:S(2)}, u32[]{:S(2)}) collective-permute-start(f32[1,24,768]{2,0,1:T(1,128)S(1)} %bitcast.99), channel_id=1, source_target_pairs={{0,1},{1,2},{2,3},{3,4},{4,5},{5,6},{6,7},{7,8},{8,9},{9,10},{10,1... | collective-permute-start | bytes 221192 | tf_op jit(solution)/shard_map/ppermute | solution.py:14
  101.8 1.3 reduce.20
  103.2 2.1 %reshape.850 = f32[768,4,24]{2,1,0:T(4,128)S(1)} reshape(f32[32,2304]{1,0:T(8,128)S(1)} %reduce.20) | data formatting | bytes 589824
  105.2 0.9 copy.464
  106.1 0.9 all_to_all.45
  107.0 1.8 %fusion.50 = (f32[4,24,768]{2,1,0:T(8,128)S(1)}, f32[4,24,768]{2,1,0:T(8,128)S(1)}) fusion(f32[4,24,768]{2,1,0:T(8,128)S(1)} %all_to_all.45, f32[4,24,767]{2,1,0:T(8,128)} %copy.461, f32[4,24,1]{2,1,0:T(8,128)} %copy.462, f32[4,24,1]{2,1,0:T(8,128)} %copy.459, f32[4,24,767]{2,1,0:T(8,128)} %copy.460, f32[4,24,768]{2,0,1:T(4,128)S(1)} %bitcast.81), kind=kLoop, calls=%fused_computation.75 | loop fusion | flops 4055040 | bytes 1769472 | tf_op jit(solution)/shard_map/mul | solution.py:68
  108.8 2.0 %fusion.28 = (f32[4,24,768]{2,1,0:T(8,128)S(1)}, f32[4,24,768]{2,1,0:T(8,128)S(1)}, f32[4,24,768]{2,1,0:T(8,128)S(1)}, f32[4,24,768]{2,1,0:T(8,128)S(1)}, f32[4,24,768]{2,1,0:T(8,128)S(1)}) fusion(f32[4,24,768]{2,1,0:T(8,128)S(1)} %all_to_all.45, f32[4,24,768]{2,1,0:T(8,128)S(1)} %get-tuple-element.119), kind=kLoop, calls=%fused_computation.53 | loop fusion | flops 15482880 | bytes 2064384 | tf_op jit(solution)/shard_map/mul | solution.py:68
  111.5 1.1 fusion.53
  115.2 5.6 %collective-permute-start.4 = (f32[3,24,768]{2,1,0:T(8,128)S(1)}, f32[3,24,768]{2,1,0:T(8,128)S(1)}, u32[]{:S(2)}, u32[]{:S(2)}) collective-permute-start(f32[3,24,768]{2,1,0:T(8,128)S(1)} %slice.519), channel_id=1, source_target_pairs={{0,1},{1,2},{2,3},{3,4},{4,5},{5,6},{6,7},{7,8},{8,9},{9,10},{10,1... | collective-permute-start | bytes 663560 | tf_op jit(solution)/shard_map/ppermute | solution.py:14
  120.8 2.8 %collective-permute-done.4 = f32[3,24,768]{2,1,0:T(8,128)S(1)} collective-permute-done((f32[3,24,768]{2,1,0:T(8,128)S(1)}, f32[3,24,768]{2,1,0:T(8,128)S(1)}, u32[]{:S(2)}, u32[]{:S(2)}) %collective-permute-start.4) | collective-permute-done | bytes 221216 | tf_op jit(solution)/shard_map/ppermute | solution.py:14
  123.7 1.9 %collective-permute-start.5 = (f32[3,24,768]{2,1,0:T(8,128)S(1)}, f32[3,24,768]{2,1,0:T(8,128)S(1)}, u32[]{:S(2)}, u32[]{:S(2)}) collective-permute-start(f32[3,24,768]{2,1,0:T(8,128)S(1)} %get-tuple-element.122), channel_id=1, source_target_pairs={{1,0},{2,1},{3,2},{4,3},{5,4},{6,5},{7,6},{8,7},{9,8},{10,9},{11,1... | collective-permute-start | bytes 663560 | tf_op jit(solution)/shard_map/ppermute | solution.py:15
  125.6 10.0 %collective-permute-done.5 = f32[3,24,768]{2,1,0:T(8,128)S(1)} collective-permute-done((f32[3,24,768]{2,1,0:T(8,128)S(1)}, f32[3,24,768]{2,1,0:T(8,128)S(1)}, u32[]{:S(2)}, u32[]{:S(2)}) %collective-permute-start.5) | collective-permute-done | bytes 221216 | tf_op jit(solution)/shard_map/ppermute | solution.py:15
  135.6 1.7 %fusion.226 = f32[4,24,768]{2,1,0:T(8,128)} fusion(f32[4,24,768]{2,1,0:T(8,128)} %copy-done.2, f32[3,24,768]{2,1,0:T(8,128)S(1)} %collective-permute-done.5), kind=kLoop, calls=%fused_computation.310 | loop fusion | flops 55296 | bytes 663552 | tf_op jit(solution)/shard_map/scatter-add | solution.py:83
  (96 shorter events, 18.3 us)
Async XLA Ops:
  24.3 18.0 %collective-permute-start = (f32[1,4,1,256]{3,2,1,0:T(1,128)S(1)}, f32[1,4,1,256]{3,2,1,0:T(1,128)S(1)}, u32[]{:S(2)}, u32[]{:S(2)}) collective-permute-start(f32[1,4,1,256]{3,2,1,0:T(1,128)S(1)} %slice.470), channel_id=1, source_target_pairs={{16,0},{32,16},{48,32},{64,48},{80,64},{96,80},{112,96},{128,112},... | collective-permute-start | bytes 12296 | tf_op jit(solution)/shard_map/ppermute | solution.py:23
  38.4 13.5 %all-to-all-start.2 = ((f32[32,1,512]{2,1,0:T(1,128)}), f32[32,1,512]{2,1,0:T(1,128)S(1)}, u32[]{:S(2)}, u32[]{:S(2)}) async-start(f32[32,1,512]{2,1,0:T(1,128)} %reshape.851), calls=%async_computation.2 | async-start | bytes 131072 | tf_op jit(solution)/shard_map/all_to_all | solution.py:99
  42.6 1.9 %copy-start = (f32[4,24,768]{2,1,0:T(8,128)S(1)}, f32[4,24,768]{2,1,0:T(8,128)}, u32[]{:S(2)}) copy-start(f32[4,24,768]{2,1,0:T(8,128)} %param.20) | copy-start | bytes 884740
  51.9 49.9 %all-to-all-start.1 = ((f32[32,1,2304]{2,1,0:T(1,128)}), f32[32,1,2304]{2,1,0:T(1,128)S(1)}, u32[]{:S(2)}, u32[]{:S(2)}) async-start(f32[32,1,2304]{2,1,0:T(1,128)} %reshape.849), calls=%async_computation.1 | async-start | bytes 589824 | tf_op jit(solution)/shard_map/all_to_all | solution.py:97
  70.0 16.1 %collective-permute-start.1 = (f32[2,4,1,768]{3,1,2,0:T(4,128)S(1)}, f32[2,4,1,768]{3,1,2,0:T(4,128)S(1)}, u32[]{:S(2)}, u32[]{:S(2)}) collective-permute-start(f32[2,4,1,768]{3,1,2,0:T(4,128)S(1)} %copy.428), channel_id=1, source_target_pairs={{16,0},{32,16},{48,32},{64,48},{80,64},{96,80},{112,96},{128,112},... | collective-permute-start | bytes 73736 | tf_op jit(solution)/shard_map/ppermute | solution.py:23
  87.6 13.6 %collective-permute-start.2 = (f32[1,24,768]{2,0,1:T(1,128)S(1)}, f32[1,24,768]{2,0,1:T(1,128)S(1)}, u32[]{:S(2)}, u32[]{:S(2)}) collective-permute-start(f32[1,24,768]{2,0,1:T(1,128)S(1)} %bitcast.98), channel_id=1, source_target_pairs={{1,0},{2,1},{3,2},{4,3},{5,4},{6,5},{7,6},{8,7},{9,8},{10,9},{11,1... | collective-permute-start | bytes 221192 | tf_op jit(solution)/shard_map/ppermute | solution.py:15
  91.6 9.6 %collective-permute-start.3 = (f32[1,24,768]{2,0,1:T(1,128)S(1)}, f32[1,24,768]{2,0,1:T(1,128)S(1)}, u32[]{:S(2)}, u32[]{:S(2)}) collective-permute-start(f32[1,24,768]{2,0,1:T(1,128)S(1)} %bitcast.99), channel_id=1, source_target_pairs={{0,1},{1,2},{2,3},{3,4},{4,5},{5,6},{6,7},{7,8},{8,9},{9,10},{10,1... | collective-permute-start | bytes 221192 | tf_op jit(solution)/shard_map/ppermute | solution.py:14
  107.0 4.5 %copy-start.1 = (f32[4,24,768]{2,1,0:T(8,128)S(1)}, f32[4,24,768]{2,1,0:T(8,128)}, u32[]{:S(2)}) copy-start(f32[4,24,768]{2,1,0:T(8,128)} %copy.443) | copy-start | bytes 884740
  107.0 4.5 %copy-start.3 = (f32[1,24,768]{2,1,0:T(8,128)S(1)}, f32[1,24,768]{2,1,0:T(8,128)}, u32[]{:S(2)}) copy-start(f32[1,24,768]{2,1,0:T(8,128)} %copy.450) | copy-start | bytes 221188
  115.2 8.4 %collective-permute-start.4 = (f32[3,24,768]{2,1,0:T(8,128)S(1)}, f32[3,24,768]{2,1,0:T(8,128)S(1)}, u32[]{:S(2)}, u32[]{:S(2)}) collective-permute-start(f32[3,24,768]{2,1,0:T(8,128)S(1)} %slice.519), channel_id=1, source_target_pairs={{0,1},{1,2},{2,3},{3,4},{4,5},{5,6},{6,7},{7,8},{8,9},{9,10},{10,1... | collective-permute-start | bytes 663560 | tf_op jit(solution)/shard_map/ppermute | solution.py:14
  123.7 11.9 %copy-start.2 = (f32[4,24,768]{2,1,0:T(8,128)}, f32[4,24,768]{2,1,0:T(8,128)S(1)}, u32[]{:S(2)}) copy-start(f32[4,24,768]{2,1,0:T(8,128)S(1)} %get-tuple-element.123) | copy-start | bytes 884740
  123.7 11.9 %collective-permute-start.5 = (f32[3,24,768]{2,1,0:T(8,128)S(1)}, f32[3,24,768]{2,1,0:T(8,128)S(1)}, u32[]{:S(2)}, u32[]{:S(2)}) collective-permute-start(f32[3,24,768]{2,1,0:T(8,128)S(1)} %get-tuple-element.122), channel_id=1, source_target_pairs={{1,0},{2,1},{3,2},{4,3},{5,4},{6,5},{7,6},{8,7},{9,8},{10,9},{11,1... | collective-permute-start | bytes 663560 | tf_op jit(solution)/shard_map/ppermute | solution.py:15
where the time goes:
time: 138 us; the launch traced here: 137 us
  starting transfers between devices  48.5 us (35%)
  local copies, waits for them, and re-layouts  37.4 us (27%)
  blocking collectives  20.6 us (15%)
  other arithmetic  17.3 us (13%)
  waiting for transfers between devices  12.8 us (9%)
    all_to_all x1, blocking collectives, local(): lax.all_to_all(velocity, 'gz', split_axis=1, concat_axis=3, tiled=True)  20.6 us
    ppermute x2, starting transfers between devices, passed_along(): return lax.ppermute(block, axis, route)  18 us
    unnamed x19, local copies, waits for them, and re-layouts  12.5 us
    ppermute x2, starting transfers between devices, padded_2(): before = lax.ppermute(last, axis, up)  11.2 us
    ppermute x2, waiting for transfers between devices, padded_2(): after = lax.ppermute(initial, axis, down)  9.98 us
    all_to_all x1, starting transfers between devices, local(): lax.all_to_all(turned, 'gy', split_axis=1, concat_axis=2, tiled=True)  9.69 us
    concatenate x3, local copies, waits for them, and re-layouts, local(): jnp.concatenate([y_refined[:, :, 1:, :], next_col], axis=2)  7.12 us
    mul x4, other arithmetic, sweep_periodic(): field * kernel_weight(offset - moved)  6.38 us
  transfers between devices with their start and end apart: 8, of which 2 were waited for; matrix products, arithmetic and copies ran while one was open for 26% of the time, Pallas kernels for 0%

commit v1 on v0

v1 whole, which is shorter than its diff:
```python
import functools

import jax
import jax.numpy as jnp
from jax import lax
from jax.experimental import pallas as pl
from jax.experimental.pallas import tpu as pltpu
from jax.sharding import PartitionSpec as P

MESH = pl.DeviceIdType.MESH
F32 = jnp.float32
BF16 = jnp.bfloat16
NGY = 32
NGZ = 16
PLANES = 4
ROWS = 24
NX = 768
LANES = 128
TILES = NX // LANES


def copy_to(src, dst, send, recv, gy, gz):
    return pltpu.make_async_remote_copy(
        src, dst, send, recv, device_id={"gy": gy, "gz": gz}, device_id_type=MESH
    )


def wait_for(ref, sem):
    pltpu.make_async_copy(ref, ref, sem).wait()


def moved_by(speed, before, after):
    half = jnp.abs(0.5 * speed)
    return speed + half * (jnp.where(speed >= 0.0, after, before) - speed)


def products(q, d):
    a = jnp.abs(d)
    b = 1.0 - a
    w = a * b
    p3 = (w * (a * a)) * (7.0 / 24.0 - (5.0 / 24.0) * a)
    pm2 = w * (1.0 / 12.0 + a * (1.0 / 24.0 + a * (-1.0 / 3.0 + (5.0 / 24.0) * a)))
    p2 = w * (-1.0 / 12.0 + a * (-1.0 / 8.0 + a * (-3.0 / 2.0 + (25.0 / 24.0) * a)))
    pm1 = w * (-2.0 / 3.0 + (a * a) * (13.0 / 8.0 - (25.0 / 24.0) * a))
    p1 = a + pm1 + 2.0 * (pm2 - p2) - 3.0 * p3
    p0 = 1.0 - (p1 + pm1) - (p2 + pm2) - p3
    right = d >= 0.0
    q0, q1, qm1, q2, qm2, q3 = (q * p for p in (p0, p1, pm1, p2, pm2, p3))
    return {
        0: q0,
        1: jnp.where(right, q1, qm1),
        -1: jnp.where(right, qm1, q1),
        2: jnp.where(right, q2, qm2),
        -2: jnp.where(right, qm2, q2),
        3: jnp.where(right, q3, 0.0),
        -3: jnp.where(right, 0.0, q3),
    }


def lane_roll(value, amount):
    amount = amount % value.shape[-1]
    return value if amount == 0 else pltpu.roll(value, amount, value.ndim - 1)


def row_roll(value, amount):
    amount = amount % value.shape[0]
    return value if amount == 0 else pltpu.roll(value, amount, 0)


def kernel(
    scalar_ref,
    vel_ref,
    out_ref,
    packed,
    send_v,
    send_n,
    send_p,
    recv_v,
    recv_n,
    recv_p,
    hal_up,
    hal_dn,
    got_up,
    got_dn,
    refine,
    coarse,
    scal,
    fine,
    field,
    edge,
    own,
    cross,
    part,
    recv_d,
    t_own,
    t_cross,
    recv_o,
    recv_c,
    sems,
):
    gy, gz = lax.axis_index("gy"), lax.axis_index("gz")
    odd = gz % 2
    next_y, prev_y = (gy + 1) % NGY, (gy + NGY - 1) % NGY
    partner = gz + 1 - 2 * odd
    other = gz - 1 + 2 * odd
    has_other = jnp.logical_and(other >= 0, other < NGZ)
    n_other = has_other.astype(jnp.int32)
    lane = lax.broadcasted_iota(jnp.int32, (8, LANES), 1)

    barrier = pltpu.get_barrier_semaphore()

    def greet(y, z):
        pl.semaphore_signal(
            barrier, inc=1, device_id={"gy": y, "gz": z}, device_id_type=MESH
        )

    def greet_z(i, _):
        greet(gy, (gz + i) % NGZ)
        return _

    def greet_zn(i, _):
        greet(next_y, (gz + i) % NGZ)
        greet(prev_y, (gz + i) % NGZ)
        return _

    def greet_y(i, _):
        greet((gy + i) % NGY, gz)
        return _

    def greet_o(i, _):
        greet((gy + i) % NGY, other)
        return _

    lax.fori_loop(1, NGZ, greet_z, 0)
    lax.fori_loop(0, NGZ, greet_zn, 0)
    lax.fori_loop(2, NGY - 1, greet_y, 0)

    @pl.when(has_other)
    def _():
        lax.fori_loop(2, NGY - 1, greet_o, 0)

    for group in range(24):
        total = jnp.zeros((8, LANES), F32)
        for y in range(8):
            rows = vel_ref[pl.ds(group * 64 + y, 8, stride=8), :]
            wide = jnp.concatenate([rows, jnp.zeros((8, LANES - 16), F32)], axis=1)
            total = total + lane_roll(wide, 16 * y)
        packed[8 + group * 8 : 16 + group * 8, :] = total
    for z in range(NGZ):
        send_v[z, 0:4, :] = packed[8 + 4 * z : 12 + 4 * z, :]
        send_v[z, 4:8, :] = packed[72 + 4 * z : 76 + 4 * z, :]
        up = packed[135 + 4 * z : 141 + 4 * z, :] if z < NGZ - 1 else packed[135 + 4 * z : 140 + 4 * z, :]
        if z == 0:
            row = lax.broadcasted_iota(jnp.int32, up.shape, 0)
            up = jnp.where(row == 0, 0.0, up)
        if z == NGZ - 1:
            send_v[z, 8:13, :] = up
            send_v[z, 13:14, :] = jnp.zeros((1, LANES), F32)
        else:
            send_v[z, 8:14, :] = up
    lane4 = lax.broadcasted_iota(jnp.int32, (4, LANES), 1)
    for z in range(NGZ):
        first = jnp.zeros((4, LANES), F32)
        last = jnp.zeros((4, LANES), F32)
        for q in range(4):
            if q < 3:
                rows = send_v[z, 4 * q : 4 * q + 4, :]
            else:
                rows = jnp.concatenate(
                    [send_v[z, 12:14, :], jnp.zeros((2, LANES), F32)], axis=0
                )
            here = jnp.logical_and(lane4 >= 32 * q, lane4 < 32 * q + 32)
            first = jnp.where(here, lane_roll(rows, 32 * q), first)
            if q < 2:
                last = jnp.where(here, lane_roll(rows, 32 + 32 * q), last)
        send_n[z] = first
        send_p[z] = last
    for k in range(3):
        for z in range(PLANES):
            hal_up[4 * k + z : 4 * k + z + 1, :] = scalar_ref[z, k : k + 1, :]
            hal_dn[4 * k + z : 4 * k + z + 1, :] = scalar_ref[z, 21 + k : 22 + k, :]
    for z in range(PLANES):
        for t in range(TILES):
            scal[t, ROWS * z : ROWS * z + ROWS, :] = scalar_ref[
                z, :, LANES * t : LANES * t + LANES
            ]
    for block in range(16):
        r = lax.broadcasted_iota(jnp.int32, (16, NX), 0) + 16 * block
        c = lax.broadcasted_iota(jnp.int32, (16, NX), 1)
        t = jnp.abs(c - 3 * r)
        if block == 0:
            t = jnp.where(r == 0, jnp.minimum(t, jnp.abs(c - NX)), t)
        refine[16 * block : 16 * block + 16, :] = (
            jnp.maximum(3 - t, 0).astype(F32).astype(BF16)
        )

    pl.semaphore_wait(barrier, 105 - 29 + 29 * n_other)

    def send_z(i, _):
        z = (gz + i) % NGZ
        copy_to(send_v.at[z], recv_v.at[gz], sems.at[0], sems.at[1], gy, z).start()
        return _

    def send_zn(i, _):
        z = (gz + i) % NGZ
        copy_to(send_n.at[z], recv_n.at[gz], sems.at[2], sems.at[3], prev_y, z).start()
        copy_to(send_p.at[z], recv_p.at[gz], sems.at[4], sems.at[5], next_y, z).start()
        return _

    lax.fori_loop(1, NGZ, send_z, 0)
    lax.fori_loop(0, NGZ, send_zn, 0)
    to_prev = copy_to(hal_up, got_dn, sems.at[6], sems.at[7], prev_y, gz)
    to_next = copy_to(hal_dn, got_up, sems.at[8], sems.at[9], next_y, gz)
    to_prev.start()
    to_next.start()
    recv_v[gz] = send_v[gz]

    wait_for(recv_v.at[0:15], sems.at[1])
    wait_for(recv_n, sems.at[3])
    wait_for(recv_p, sems.at[5])

    for c in range(8):
        for half in range(2):
            top = jnp.zeros((8, LANES), F32)
            low = jnp.zeros((6, LANES), F32)
            for i in range(8):
                g = 8 * half + i
                here = jnp.logical_and(lane >= 16 * i, lane < 16 * i + 16)
                top = jnp.where(here, lane_roll(recv_v[g, 0:8, :], 16 * (i - c)), top)
                low = jnp.where(
                    here[0:6], lane_roll(recv_v[g, 8:14, :], 16 * (i - c)), low
                )
            base = 16 * (c + 2)
            columns = pl.ds(LANES * half, LANES)
            coarse[base : base + 8, columns] = top
            coarse[base + 8 : base + 14, columns] = low
            coarse[base + 14 : base + 16, columns] = jnp.zeros((2, LANES), F32)
    for c in (-2, -1, 8, 9):
        source, offset, chunks = (recv_n, c - 8, 4) if c > 0 else (recv_p, c + 2, 2)
        base = 16 * (c + 2)
        for half in range(2):
            columns = pl.ds(LANES * half, LANES)
            for q in range(4):
                total = jnp.zeros((4, LANES), F32)
                if q < chunks:
                    for i in range(8):
                        here = jnp.logical_and(lane4 >= 16 * i, lane4 < 16 * i + 16)
                        rows = source[8 * half + i]
                        total = jnp.where(
                            here, lane_roll(rows, 16 * i - 32 * q - 16 * offset), total
                        )
                coarse[base + 4 * q : base + 4 * q + 4, columns] = total
    value = coarse[...]
    high = value.astype(BF16)
    low = (value - high.astype(F32)).astype(BF16)
    for pair in range(TILES // 2):
        weights = refine[:, 2 * LANES * pair : 2 * LANES * (pair + 1)]
        result = (
            jnp.dot(high, weights, preferred_element_type=F32)
            + jnp.dot(low, weights, preferred_element_type=F32)
        ) * (1.0 / 3.0)
        fine[2 * pair] = result[:, :LANES]
        fine[2 * pair + 1] = result[:, LANES:]

    def level(first, plane, t):
        return fine[t, pl.ds(16 * (first + 2) + plane, 8, stride=16), :]

    def edge_level(shift, plane, t):
        return jnp.concatenate(
            [
                fine[t, pl.ds(16 * (1 + shift) + plane, 4), :],
                fine[t, pl.ds(16 * (10 + shift) + plane, 4), :],
            ],
            axis=0,
        )

    def whole(load):
        return jnp.concatenate([load(t) for t in range(TILES)], axis=1)

    def spread(ref, rows, value):
        for t in range(TILES):
            ref[t, rows, :] = value[:, LANES * t : LANES * t + LANES]

    def mixed(base, following, k):
        return base if k == 0 else base * (1.0 - k / 3.0) + following * (k / 3.0)

    def sweep_x(q, u):
        d = moved_by(u, lane_roll(u, 1), lane_roll(u, -1))
        terms = products(q, d)
        total = terms[0]
        for m in (-3, -2, -1, 1, 2, 3):
            total = total + lane_roll(terms[m], m)
        return total

    for z in range(PLANES):
        base = whole(functools.partial(level, 0, z))
        following = whole(functools.partial(level, 1, z))
        for k in range(3):
            q = whole(lambda t: scal[t, pl.ds(ROWS * z + k, 8, stride=3), :])
            i = 8 * (3 * z + k)
            spread(field, slice(i, i + 8), sweep_x(q, mixed(base, following, k)))
    wait_for(got_up, sems.at[7])
    wait_for(got_dn, sems.at[9])
    base = whole(functools.partial(edge_level, 0, 0))
    following = whole(functools.partial(edge_level, 1, 0))
    for k in range(3):
        q = jnp.concatenate(
            [got_up[4 * k : 4 * k + 4, :], got_dn[4 * k : 4 * k + 4, :]], axis=0
        )
        spread(
            edge, slice(8 * k, 8 * k + 8), sweep_x(q, mixed(base, following, k))
        )

    row = lax.broadcasted_iota(jnp.int32, (8, LANES), 0)

    def phases(before, base, following, q_of):
        u = [mixed(base, following, k) for k in range(3)]
        sides = [mixed(before, base, 2)] + u + [following]
        sums = {}
        for k in range(3):
            terms = products(q_of(k), moved_by(u[k], sides[k], sides[k + 2]))
            for m in range(-3, 4):
                key = ((k + m) % 3, (k + m) // 3)
                sums[key] = terms[m] if key not in sums else sums[key] + terms[m]
        return sums

    def tile_step(t, _):
        edges = phases(
            edge_level(-1, 4, t),
            edge_level(0, 4, t),
            edge_level(1, 4, t),
            lambda k: edge[t, 8 * k : 8 * k + 8, :],
        )
        swept = {}
        for z in range(PLANES):
            sums = phases(
                level(-1, 4 + z, t),
                level(0, 4 + z, t),
                level(1, 4 + z, t),
                lambda k: field[t, 8 * (3 * z + k) : 8 * (3 * z + k) + 8, :],
            )
            for k in range(3):
                above = jnp.where(
                    row == 0, row_roll(edges[k, 1], -z), row_roll(sums[k, 1], 1)
                )
                below = jnp.where(
                    row == 7, row_roll(edges[k, -1], 3 - z), row_roll(sums[k, -1], -1)
                )
                swept[z, k] = sums[k, 0] + above + below
        lower = [level(0, 8 + p, t) for p in range(6)]
        upper = [level(1, 8 + p, t) for p in range(6)]
        for k in range(3):
            u = [mixed(lower[p], upper[p], k) for p in range(6)]
            sums = {}
            for z in range(PLANES):
                terms = products(swept[z, k], moved_by(u[z + 1], u[z], u[z + 2]))
                for m in range(-3, 4):
                    sums[z + m] = terms[m] if z + m not in sums else sums[z + m] + terms[m]
            for z in range(PLANES):
                own[t, pl.ds(ROWS * z + k, 8, stride=3), :] = sums[z]
            for i in range(3):
                up, down = sums[4 + i], sums[i - 3]
                cross[t, pl.ds(ROWS * i + k, 8, stride=3), :] = jnp.where(
                    odd == 1, up, down
                )
                part[t, pl.ds(ROWS * i + k, 8, stride=3), :] = jnp.where(
                    odd == 1, down, up
                )
        return _

    lax.fori_loop(0, TILES, tile_step, 0)

    to_partner = copy_to(part, recv_d, sems.at[10], sems.at[11], gy, partner)
    to_partner.start()

    def transposed(source, target):
        for t in range(TILES):
            target[LANES * t : LANES * t + LANES, :] = source[t].T

    def dest(i):
        y = (gy + i) % NGY
        return y, pl.ds(pl.multiple_of(ROWS * y, 8), ROWS)

    @pl.when(has_other)
    def _():
        transposed(cross, t_cross)

        def send(i, _):
            y, rows = dest(i)
            copy_to(
                t_cross.at[rows], recv_c.at[gy], sems.at[12], sems.at[13], y, other
            ).start()
            return _

        lax.fori_loop(0, NGY, send, 0)

    wait_for(recv_d, sems.at[11])
    target = pl.ds(pl.multiple_of(ROWS * odd_to_first(odd), 8), 72)
    own[:, target, :] = own[:, target, :] + recv_d[...]
    transposed(own, t_own)

    def send_own(i, _):
        y, rows = dest(i)
        copy_to(t_own.at[rows], recv_o.at[gy], sems.at[14], sems.at[15], y, gz).start()
        return _

    lax.fori_loop(1, NGY, send_own, 0)
    recv_o[gy] = t_own[pl.ds(pl.multiple_of(ROWS * gy, 8), ROWS), :]

    @pl.when(has_other)
    def _():
        wait_for(recv_c, sems.at[13])

    @pl.when(jnp.logical_not(has_other))
    def _():
        recv_c[...] = jnp.zeros_like(recv_c)

    wait_for(recv_o.at[0 : NGY - 1], sems.at[15])

    keep = lane < 3 * ROWS

    for x in range(3):
        rows = pl.ds(8 * x, 8)
        totals = {}
        for y in range(NGY):
            extra = jnp.where(keep, recv_c[y, rows, :], 0.0)
            moved = lane_roll(extra, ROWS)
            value = recv_o[y, rows, :] + jnp.where(odd == 1, moved, extra)
            start = ROWS * y
            for z in range(PLANES):
                turned = lane_roll(value, ROWS * (y - z))
                for t in range(start // LANES, (start + ROWS - 1) // LANES + 1):
                    at = lane + LANES * t
                    here = jnp.logical_and(at >= start, at < start + ROWS)
                    old = totals.get((z, t))
                    totals[z, t] = (
                        turned if old is None else jnp.where(here, turned, old)
                    )
            for t in range(TILES):
                if (t + 1) * LANES <= start + ROWS and (0, t) in totals:
                    for z in range(PLANES):
                        out_ref[z, rows, LANES * t : LANES * t + LANES] = totals.pop(
                            (z, t)
                        )

    wait_for(send_v.at[0:15], sems.at[0])
    wait_for(send_n, sems.at[2])
    wait_for(send_p, sems.at[4])
    wait_for(hal_up, sems.at[6])
    wait_for(hal_dn, sems.at[8])
    wait_for(part, sems.at[10])
    wait_for(recv_o.at[0 : NGY - 1], sems.at[14])

    @pl.when(has_other)
    def _():
        wait_for(recv_c, sems.at[12])


def odd_to_first(odd):
    return 1 - odd


def local(scalar, velocity):
    vmem = pl.BlockSpec(memory_space=pltpu.VMEM)
    buffers = [
        (208, LANES),
        (NGZ, 14, LANES),
        (NGZ, 4, LANES),
        (NGZ, 4, LANES),
        (NGZ, 14, LANES),
        (NGZ, 4, LANES),
        (NGZ, 4, LANES),
        (12, NX),
        (12, NX),
        (12, NX),
        (12, NX),
    ]
    later = [
        (192, 256),
        (TILES, 96, LANES),
        (TILES, 192, LANES),
        (TILES, 96, LANES),
        (TILES, 24, LANES),
        (TILES, LANES, LANES),
        (TILES, LANES, LANES),
        (TILES, 72, LANES),
        (TILES, 72, LANES),
        (NX, LANES),
        (NX, LANES),
        (NGY, ROWS, LANES),
        (NGY, ROWS, LANES),
    ]
    return pl.pallas_call(
        kernel,
        out_shape=jax.ShapeDtypeStruct((PLANES, ROWS, NX), F32),
        in_specs=[vmem, vmem],
        out_specs=vmem,
        scratch_shapes=[pltpu.VMEM(s, F32) for s in buffers]
        + [pltpu.VMEM((256, NX), BF16)]
        + [pltpu.VMEM(s, F32) for s in later]
        + [pltpu.SemaphoreType.DMA((16,))],
        compiler_params=pltpu.CompilerParams(collective_id=0, has_side_effects=True),
    )(scalar, velocity.reshape(3 * 64 * 8, 16))


def solution(mesh):
    in_specs = (P("gz", "gy", None), P(None, None, "gy", "gz"))
    out_specs = P("gz", "gy", None)
    return jax.shard_map(
        local, mesh=mesh, in_specs=in_specs, out_specs=out_specs, check_vma=False
    )
```

time: 138 us -> 73.2 us (0.53)
  the two profiles are of different devices: /device:TPU:1 before, /device:TPU:51 now
where the time goes in v1:
time: 73.2 us; the launch traced here: 73 us
  Pallas kernels  69.2 us (95%)
  local copies, waits for them, and re-layouts  3.78 us (5%)
    pallas_call x1, Pallas kernels, local(): pl.pallas_call(kernel, out_shape=jax.ShapeDtypeStruct((PLANES, ROWS, NX),...  69.2 us
    unnamed x2, local copies, waits for them, and re-layouts  3.78 us

profile of v1, /device:TPU:51, one launch (start us, length us, event | category | flops | bytes accessed | tf_op | source)
XLA Modules:
  0.0 73.0 jit_solution(5531779933346848762)
XLA Ops:
  0.0 2.1 %copy.3 = f32[3,64,8,16]{3,2,1,0:T(8,128)} copy(f32[3,64,8,16]{1,3,2,0:T(8,128)} %param.3) | data formatting | bytes 196608 | tf_op args[1]
  2.1 69.2 %shard_map.28 = f32[4,24,768]{2,1,0:T(8,128)} custom-call(f32[4,24,768]{2,1,0:T(8,128)} %scalar_ref.1, f32[1536,16]{1,0:T(8,128)} %bitcast.1), custom_call_target="tpu_custom_call" | custom-call | tf_op jit(solution)/shard_map/pallas_call | solution.py:493
  71.3 1.7 %copy.5 = f32[4,24,768]{2,1,0:T(8,128)} copy(f32[4,24,768]{2,1,0:T(8,128)} %shard_map.28) | data formatting | bytes 589824

commit v2 on v1

--- a/solution.py
+++ b/solution.py
@@ -65,6 +65,11 @@
 def row_roll(value, amount):
     amount = amount % value.shape[0]
     return value if amount == 0 else pltpu.roll(value, amount, 0)
+
+
+def offset_of(i):
+    half = (i + 1) // 2
+    return half * (2 * (i % 2) - 1) + NGY
 
 
 def kernel(
@@ -94,8 +99,11 @@
     recv_d,
     t_own,
     t_cross,
+    send_o,
+    send_c,
     recv_o,
     recv_c,
+    joined,
     sems,
 ):
     gy, gz = lax.axis_index("gy"), lax.axis_index("gz")
@@ -139,13 +147,8 @@
     def _():
         lax.fori_loop(2, NGY - 1, greet_o, 0)
 
-    for group in range(24):
-        total = jnp.zeros((8, LANES), F32)
-        for y in range(8):
-            rows = vel_ref[pl.ds(group * 64 + y, 8, stride=8), :]
-            wide = jnp.concatenate([rows, jnp.zeros((8, LANES - 16), F32)], axis=1)
-            total = total + lane_roll(wide, 16 * y)
-        packed[8 + group * 8 : 16 + group * 8, :] = total
+    for i in range(3):
+        packed[8 + 64 * i : 72 + 64 * i, :] = vel_ref[i].T
     for z in range(NGZ):
         send_v[z, 0:4, :] = packed[8 + 4 * z : 12 + 4 * z, :]
         send_v[z, 4:8, :] = packed[72 + 4 * z : 76 + 4 * z, :]
@@ -184,6 +187,10 @@
             scal[t, ROWS * z : ROWS * z + ROWS, :] = scalar_ref[
                 z, :, LANES * t : LANES * t + LANES
             ]
+    @pl.when(jnp.logical_not(has_other))
+    def _():
+        recv_c[...] = jnp.zeros_like(recv_c)
+
     for block in range(16):
         r = lax.broadcasted_iota(jnp.int32, (16, NX), 0) + 16 * block
         c = lax.broadcasted_iota(jnp.int32, (16, NX), 1)
@@ -197,12 +204,12 @@
     pl.semaphore_wait(barrier, 105 - 29 + 29 * n_other)
 
     def send_z(i, _):
-        z = (gz + i) % NGZ
+        z = (gz + offset_of(i)) % NGZ
         copy_to(send_v.at[z], recv_v.at[gz], sems.at[0], sems.at[1], gy, z).start()
         return _
 
     def send_zn(i, _):
-        z = (gz + i) % NGZ
+        z = (gz + offset_of(i)) % NGZ
         copy_to(send_n.at[z], recv_n.at[gz], sems.at[2], sems.at[3], prev_y, z).start()
         copy_to(send_p.at[z], recv_p.at[gz], sems.at[4], sems.at[5], next_y, z).start()
         return _
@@ -377,71 +384,111 @@
         for t in range(TILES):
             target[LANES * t : LANES * t + LANES, :] = source[t].T
 
-    def dest(i):
-        y = (gy + i) % NGY
-        return y, pl.ds(pl.multiple_of(ROWS * y, 8), ROWS)
+    def rows_of(ref, y):
+        base = ROWS * y
+        return [
+            ref[pl.ds(pl.multiple_of(base + 8 * i, 8), 8), :] for i in range(3)
+        ]
 
     @pl.when(has_other)
     def _():
         transposed(cross, t_cross)
 
+        def pack(y, _):
+            v = rows_of(t_cross, y)
+            send_c[y, 0:8, :] = jnp.where(lane < 72, v[0], lane_roll(v[2], 72))
+            send_c[y, 8:16, :] = jnp.where(lane < 72, v[1], lane_roll(v[2], 16))
+            return _
+
+        lax.fori_loop(0, NGY, pack, 0, unroll=8)
+
         def send(i, _):
-            y, rows = dest(i)
+            y = (gy + offset_of(i)) % NGY
             copy_to(
-                t_cross.at[rows], recv_c.at[gy], sems.at[12], sems.at[13], y, other
+                send_c.at[y], recv_c.at[gy], sems.at[12], sems.at[13], y, other
             ).start()
             return _
 
         lax.fori_loop(0, NGY, send, 0)
 
     wait_for(recv_d, sems.at[11])
-    target = pl.ds(pl.multiple_of(ROWS * odd_to_first(odd), 8), 72)
+    target = pl.ds(pl.multiple_of(ROWS * (1 - odd), 8), 72)
     own[:, target, :] = own[:, target, :] + recv_d[...]
     transposed(own, t_own)
 
+    def pack_own(y, _):
+        v = rows_of(t_own, y)
+        send_o[y, 0:8, :] = jnp.where(lane < 96, v[0], lane_roll(v[2], 96))
+        send_o[y, 8:16, :] = jnp.where(lane < 96, v[1], lane_roll(v[2], 64))
+        tail = v[2]
+        tail = lane_roll(v[2], 64)
+        for q in range(1, 4):
+            piece = row_roll(lane_roll(v[2], 32 * q + 64), -2 * q)
+            tail = jnp.where(lane < 32 * q, tail, piece)
+        send_o[y, 16:18, :] = tail[0:2]
+        return _
+
+    lax.fori_loop(0, NGY, pack_own, 0, unroll=8)
+
     def send_own(i, _):
-        y, rows = dest(i)
-        copy_to(t_own.at[rows], recv_o.at[gy], sems.at[14], sems.at[15], y, gz).start()
+        y = (gy + offset_of(i)) % NGY
+        copy_to(send_o.at[y], recv_o.at[gy], sems.at[14], sems.at[15], y, gz).start()
         return _
 
     lax.fori_loop(1, NGY, send_own, 0)
-    recv_o[gy] = t_own[pl.ds(pl.multiple_of(ROWS * gy, 8), ROWS), :]
+    recv_o[gy] = send_o[gy]
 
     @pl.when(has_other)
     def _():
         wait_for(recv_c, sems.at[13])
 
-    @pl.when(jnp.logical_not(has_other))
-    def _():
-        recv_c[...] = jnp.zeros_like(recv_c)
-
     wait_for(recv_o.at[0 : NGY - 1], sems.at[15])
 
-    keep = lane < 3 * ROWS
-
-    for x in range(3):
-        rows = pl.ds(8 * x, 8)
-        totals = {}
-        for y in range(NGY):
-            extra = jnp.where(keep, recv_c[y, rows, :], 0.0)
-            moved = lane_roll(extra, ROWS)
-            value = recv_o[y, rows, :] + jnp.where(odd == 1, moved, extra)
-            start = ROWS * y
+    inside = lane - ROWS * odd
+    keep = jnp.logical_and(inside >= 0, inside < 72)
+    head = inside < 56
+
+    def add_up(y, _):
+        p0, p1 = recv_o[y, 0:8, :], recv_o[y, 8:16, :]
+        tail = recv_o[y, 16:18, :]
+        tail = jnp.concatenate([tail, tail, tail, tail], axis=0)
+        last = jnp.where(lane < 32, lane_roll(p0, 32), lane_roll(p1, 64))
+        end = lane_roll(tail, 64)
+        for q in range(1, 4):
+            end = jnp.where(row < 2 * q, end, lane_roll(tail, 64 - 32 * q))
+        last = jnp.where(lane < 64, last, end)
+        c0, c1 = recv_c[y, 0:8, :], recv_c[y, 8:16, :]
+        turn = ROWS * odd
+        e0, e1 = pltpu.roll(c0, turn, 1), pltpu.roll(c1, turn, 1)
+        e2 = jnp.where(
+            head, pltpu.roll(c0, turn + 56, 1), pltpu.roll(c1, (turn + 112) % LANES, 1)
+        )
+        joined[y, 0:8, :] = p0 + jnp.where(keep, e0, 0.0)
+        joined[y, 8:16, :] = p1 + jnp.where(keep, e1, 0.0)
+        joined[y, 16:24, :] = last + jnp.where(keep, e2, 0.0)
+        return _
+
+    lax.fori_loop(0, NGY, add_up, 0, unroll=8)
+
+    def place(x, _):
+        rows = pl.ds(pl.multiple_of(8 * x, 8), 8)
+        for t in range(TILES):
+            pieces = [None] * PLANES
+            for y in range(LANES * t // ROWS, (LANES * t + LANES - 1) // ROWS + 1):
+                value = joined[y, rows, :]
+                edge_at = ROWS * y - LANES * t
+                for z in range(PLANES):
+                    turned = lane_roll(value, ROWS * (y - z))
+                    pieces[z] = (
+                        turned
+                        if pieces[z] is None
+                        else jnp.where(lane < edge_at, pieces[z], turned)
+                    )
             for z in range(PLANES):
-                turned = lane_roll(value, ROWS * (y - z))
-                for t in range(start // LANES, (start + ROWS - 1) // LANES + 1):
-                    at = lane + LANES * t
-                    here = jnp.logical_and(at >= start, at < start + ROWS)
-                    old = totals.get((z, t))
-                    totals[z, t] = (
-                        turned if old is None else jnp.where(here, turned, old)
-                    )
-            for t in range(TILES):
-                if (t + 1) * LANES <= start + ROWS and (0, t) in totals:
-                    for z in range(PLANES):
-                        out_ref[z, rows, LANES * t : LANES * t + LANES] = totals.pop(
-                            (z, t)
-                        )
+                out_ref[z, rows, LANES * t : LANES * t + LANES] = pieces[z]
+        return _
+
+    lax.fori_loop(0, 3, place, 0)
 
     wait_for(send_v.at[0:15], sems.at[0])
     wait_for(send_n, sems.at[2])
@@ -454,10 +501,6 @@
     @pl.when(has_other)
     def _():
         wait_for(recv_c, sems.at[12])
-
-
-def odd_to_first(odd):
-    return 1 - odd
 
 
 def local(scalar, velocity):
@@ -487,7 +530,10 @@
         (TILES, 72, LANES),
         (NX, LANES),
         (NX, LANES),
-        (NGY, ROWS, LANES),
+        (NGY, 18, LANES),
+        (NGY, 16, LANES),
+        (NGY, 18, LANES),
+        (NGY, 16, LANES),
         (NGY, ROWS, LANES),
     ]
     return pl.pallas_call(
@@ -500,7 +546,7 @@
         + [pltpu.VMEM(s, F32) for s in later]
         + [pltpu.SemaphoreType.DMA((16,))],
         compiler_params=pltpu.CompilerParams(collective_id=0, has_side_effects=True),
-    )(scalar, velocity.reshape(3 * 64 * 8, 16))
+    )(scalar, velocity.transpose(0, 2, 3, 1).reshape(3, LANES, 64))
 
 
 def solution(mesh):

time: 73.2 us -> 53.1 us (0.73)
  the two profiles are of different devices: /device:TPU:51 before, /device:TPU:1 now
where the time goes in v2:
time: 53.1 us; the launch traced here: 53 us
  Pallas kernels  51.3 us (97%)
  local copies, waits for them, and re-layouts  1.69 us (3%)
    pallas_call x1, Pallas kernels, local(): pl.pallas_call(kernel, out_shape=jax.ShapeDtypeStruct((PLANES, ROWS, NX),...  51.3 us
    unnamed x1, local copies, waits for them, and re-layouts  1.69 us

profile of v2, /device:TPU:1, one launch (start us, length us, event | category | flops | bytes accessed | tf_op | source)
XLA Modules:
  0.0 53.0 jit_solution(13587201634208203217)
XLA Ops:
  0.0 51.3 %shard_map.28 = f32[4,24,768]{2,1,0:T(8,128)} custom-call(f32[4,24,768]{2,1,0:T(8,128)} %scalar_ref.1, f32[3,128,64]{2,1,0:T(8,128)} %bitcast.3), custom_call_target="tpu_custom_call" | custom-call | tf_op jit(solution)/shard_map/pallas_call | solution.py:539
  51.3 1.7 %copy.4 = f32[4,24,768]{2,1,0:T(8,128)} copy(f32[4,24,768]{2,1,0:T(8,128)} %shard_map.28) | data formatting | bytes 589824

commit v3 on v2

--- a/solution.py
+++ b/solution.py
@@ -76,6 +76,7 @@
     scalar_ref,
     vel_ref,
     out_ref,
+    vel,
     packed,
     send_v,
     send_n,
@@ -115,6 +116,13 @@
     n_other = has_other.astype(jnp.int32)
     lane = lax.broadcasted_iota(jnp.int32, (8, LANES), 1)
 
+    take_vel = pltpu.make_async_copy(vel_ref, vel, sems.at[16])
+    take_vel.start()
+    for t in range(TILES):
+        pltpu.make_async_copy(
+            scalar_ref.at[:, :, LANES * t : LANES * t + LANES], scal.at[t], sems.at[17]
+        ).start()
+
     barrier = pltpu.get_barrier_semaphore()
 
     def greet(y, z):
@@ -139,16 +147,31 @@
         greet((gy + i) % NGY, other)
         return _
 
+    lax.fori_loop(0, NGZ, greet_zn, 0)
     lax.fori_loop(1, NGZ, greet_z, 0)
-    lax.fori_loop(0, NGZ, greet_zn, 0)
     lax.fori_loop(2, NGY - 1, greet_y, 0)
 
     @pl.when(has_other)
     def _():
         lax.fori_loop(2, NGY - 1, greet_o, 0)
 
+    @pl.when(jnp.logical_not(has_other))
+    def _():
+        joined[...] = jnp.zeros_like(joined)
+
+    for block in range(16):
+        r = lax.broadcasted_iota(jnp.int32, (16, NX), 0) + 16 * block
+        c = lax.broadcasted_iota(jnp.int32, (16, NX), 1)
+        t = jnp.abs(c - 3 * r)
+        if block == 0:
+            t = jnp.where(r == 0, jnp.minimum(t, jnp.abs(c - NX)), t)
+        refine[16 * block : 16 * block + 16, :] = (
+            jnp.maximum(3 - t, 0).astype(F32).astype(BF16)
+        )
+
+    take_vel.wait()
     for i in range(3):
-        packed[8 + 64 * i : 72 + 64 * i, :] = vel_ref[i].T
+        packed[8 + 64 * i : 72 + 64 * i, :] = vel[i].T
     for z in range(NGZ):
         send_v[z, 0:4, :] = packed[8 + 4 * z : 12 + 4 * z, :]
         send_v[z, 4:8, :] = packed[72 + 4 * z : 76 + 4 * z, :]
@@ -178,28 +201,14 @@
                 last = jnp.where(here, lane_roll(rows, 32 + 32 * q), last)
         send_n[z] = first
         send_p[z] = last
-    for k in range(3):
-        for z in range(PLANES):
-            hal_up[4 * k + z : 4 * k + z + 1, :] = scalar_ref[z, k : k + 1, :]
-            hal_dn[4 * k + z : 4 * k + z + 1, :] = scalar_ref[z, 21 + k : 22 + k, :]
-    for z in range(PLANES):
-        for t in range(TILES):
-            scal[t, ROWS * z : ROWS * z + ROWS, :] = scalar_ref[
-                z, :, LANES * t : LANES * t + LANES
-            ]
-    @pl.when(jnp.logical_not(has_other))
-    def _():
-        recv_c[...] = jnp.zeros_like(recv_c)
-
-    for block in range(16):
-        r = lax.broadcasted_iota(jnp.int32, (16, NX), 0) + 16 * block
-        c = lax.broadcasted_iota(jnp.int32, (16, NX), 1)
-        t = jnp.abs(c - 3 * r)
-        if block == 0:
-            t = jnp.where(r == 0, jnp.minimum(t, jnp.abs(c - NX)), t)
-        refine[16 * block : 16 * block + 16, :] = (
-            jnp.maximum(3 - t, 0).astype(F32).astype(BF16)
-        )
+    wait_for(scal, sems.at[17])
+    for t in range(TILES):
+        columns = pl.ds(LANES * t, LANES)
+        for k in range(3):
+            for z in range(PLANES):
+                at = slice(4 * k + z, 4 * k + z + 1)
+                hal_up[at, columns] = scal[t, z, k : k + 1, :]
+                hal_dn[at, columns] = scal[t, z, 21 + k : 22 + k, :]
 
     pl.semaphore_wait(barrier, 105 - 29 + 29 * n_other)
 
@@ -299,13 +308,16 @@
             total = total + lane_roll(terms[m], m)
         return total
 
-    for z in range(PLANES):
+    def plane_x(z, _):
         base = whole(functools.partial(level, 0, z))
         following = whole(functools.partial(level, 1, z))
         for k in range(3):
-            q = whole(lambda t: scal[t, pl.ds(ROWS * z + k, 8, stride=3), :])
-            i = 8 * (3 * z + k)
-            spread(field, slice(i, i + 8), sweep_x(q, mixed(base, following, k)))
+            q = whole(lambda t: scal[t, z, pl.ds(k, 8, stride=3), :])
+            rows = pl.ds(pl.multiple_of(24 * z + 8 * k, 8), 8)
+            spread(field, rows, sweep_x(q, mixed(base, following, k)))
+        return _
+
+    lax.fori_loop(0, PLANES, plane_x, 0)
     wait_for(got_up, sems.at[7])
     wait_for(got_dn, sems.at[9])
     base = whole(functools.partial(edge_level, 0, 0))
@@ -375,14 +387,11 @@
                 )
         return _
 
-    lax.fori_loop(0, TILES, tile_step, 0)
-
-    to_partner = copy_to(part, recv_d, sems.at[10], sems.at[11], gy, partner)
-    to_partner.start()
-
-    def transposed(source, target):
-        for t in range(TILES):
-            target[LANES * t : LANES * t + LANES, :] = source[t].T
+    def transposed(source, target, h):
+        for i in range(TILES // 2):
+            t = TILES // 2 * h + i
+            rows = pl.ds(pl.multiple_of(LANES * t, LANES), LANES)
+            target[rows, :] = source[t].T
 
     def rows_of(ref, y):
         base = ROWS * y
@@ -390,63 +399,122 @@
             ref[pl.ds(pl.multiple_of(base + 8 * i, 8), 8), :] for i in range(3)
         ]
 
-    @pl.when(has_other)
-    def _():
-        transposed(cross, t_cross)
-
-        def pack(y, _):
-            v = rows_of(t_cross, y)
-            send_c[y, 0:8, :] = jnp.where(lane < 72, v[0], lane_roll(v[2], 72))
-            send_c[y, 8:16, :] = jnp.where(lane < 72, v[1], lane_roll(v[2], 16))
-            return _
-
-        lax.fori_loop(0, NGY, pack, 0, unroll=8)
-
-        def send(i, _):
-            y = (gy + offset_of(i)) % NGY
-            copy_to(
-                send_c.at[y], recv_c.at[gy], sems.at[12], sems.at[13], y, other
-            ).start()
-            return _
-
-        lax.fori_loop(0, NGY, send, 0)
-
-    wait_for(recv_d, sems.at[11])
-    target = pl.ds(pl.multiple_of(ROWS * (1 - odd), 8), 72)
-    own[:, target, :] = own[:, target, :] + recv_d[...]
-    transposed(own, t_own)
-
-    def pack_own(y, _):
+    def in_groups(pack, send, h):
+        def order(i):
+            return NGY // 2 * h + (gy + offset_of((i + 1) % 16)) % (NGY // 2)
+
+        for n in range(2):
+            for i in range(8):
+                pack(order(8 * n + i))
+            if n:
+                for i in range(8):
+                    send(order(i))
+        for i in range(8):
+            send(order(i + 8))
+
+    def pack_cross(y):
+        v = rows_of(t_cross, y)
+        send_c[y, 0:8, :] = jnp.where(lane < 72, v[0], lane_roll(v[2], 72))
+        low = jnp.where(lane < 72, v[1], lane_roll(v[2], 16))
+        low = jnp.where(lane < 88, low, row_roll(lane_roll(v[2], 32), -6))
+        for q in range(3):
+            piece = row_roll(lane_roll(v[1], 104 - 24 * q), 2 * q - 6)
+            here = lane >= 104 if q == 0 else jnp.logical_and(lane >= 104, row >= 2 * q)
+            low = jnp.where(here, piece, low)
+        send_c[y, 8:14, :] = low[0:6]
+
+    def send_cross(y):
+        copy_to(
+            send_c.at[y], recv_c.at[gy], sems.at[12], sems.at[13], y, other
+        ).start()
+
+    def pack_own(y):
         v = rows_of(t_own, y)
         send_o[y, 0:8, :] = jnp.where(lane < 96, v[0], lane_roll(v[2], 96))
         send_o[y, 8:16, :] = jnp.where(lane < 96, v[1], lane_roll(v[2], 64))
-        tail = v[2]
         tail = lane_roll(v[2], 64)
         for q in range(1, 4):
             piece = row_roll(lane_roll(v[2], 32 * q + 64), -2 * q)
             tail = jnp.where(lane < 32 * q, tail, piece)
         send_o[y, 16:18, :] = tail[0:2]
-        return _
-
-    lax.fori_loop(0, NGY, pack_own, 0, unroll=8)
-
-    def send_own(i, _):
-        y = (gy + offset_of(i)) % NGY
-        copy_to(send_o.at[y], recv_o.at[gy], sems.at[14], sems.at[15], y, gz).start()
-        return _
-
-    lax.fori_loop(1, NGY, send_own, 0)
+
+    def send_own(y):
+        @pl.when(y != gy)
+        def _():
+            copy_to(
+                send_o.at[y], recv_o.at[gy], sems.at[14], sems.at[15], y, gz
+            ).start()
+
+    def half_of(ref, h):
+        return ref.at[pl.ds(TILES // 2 * h, TILES // 2)]
+
+    def cross_step(step, carry):
+        h = (gy + step) % 2
+
+        def tiles(i, _):
+            return tile_step(TILES // 2 * h + i, _)
+
+        lax.fori_loop(0, TILES // 2, tiles, 0)
+        copy_to(
+            half_of(part, h), half_of(recv_d, h), sems.at[10], sems.at[18 + step], gy, partner
+        ).start()
+
+        @pl.when(has_other)
+        def _():
+            transposed(cross, t_cross, h)
+            in_groups(pack_cross, send_cross, h)
+
+        return carry
+
+    lax.fori_loop(0, 2, cross_step, 0)
+
+    target = pl.ds(pl.multiple_of(ROWS * (1 - odd), 8), 72)
+
+    def own_step(step, _):
+        h = (gy + step) % 2
+        wait_for(half_of(recv_d, h), sems.at[18 + step])
+        tiles = pl.ds(TILES // 2 * h, TILES // 2)
+        own[tiles, target, :] = own[tiles, target, :] + recv_d[tiles]
+        transposed(own, t_own, h)
+        in_groups(pack_own, send_own, h)
+        return _
+
+    lax.fori_loop(0, 2, own_step, 0)
     recv_o[gy] = send_o[gy]
+
+    inside = lane - ROWS * odd
+    keep = jnp.logical_and(inside >= 0, inside < 72)
+    head = inside < 56
 
     @pl.when(has_other)
     def _():
         wait_for(recv_c, sems.at[13])
 
+        turn = ROWS * odd
+
+        def turned(value, amount):
+            return pltpu.roll(value, (turn + amount) % LANES, 1)
+
+        def open_cross(y, _):
+            c0 = recv_c[y, 0:8, :]
+            c1 = jnp.concatenate(
+                [recv_c[y, 8:14, :], jnp.zeros((2, LANES), F32)], axis=0
+            )
+            tail = turned(row_roll(c1, 6), 24)
+            for q in range(1, 3):
+                piece = turned(row_roll(c1, 6 - 2 * q), 24 * q + 24)
+                tail = jnp.where(inside < 24 * q, tail, piece)
+            end = jnp.where(row < 6, turned(c1, 112), turned(row_roll(c1, 6), 96))
+            e1 = jnp.where(row < 6, turned(c1, 0), tail)
+            e2 = jnp.where(head, turned(c0, 56), end)
+            joined[y, 0:8, :] = jnp.where(keep, turned(c0, 0), 0.0)
+            joined[y, 8:16, :] = jnp.where(keep, e1, 0.0)
+            joined[y, 16:24, :] = jnp.where(keep, e2, 0.0)
+            return _
+
+        lax.fori_loop(0, NGY, open_cross, 0, unroll=8)
+
     wait_for(recv_o.at[0 : NGY - 1], sems.at[15])
-
-    inside = lane - ROWS * odd
-    keep = jnp.logical_and(inside >= 0, inside < 72)
-    head = inside < 56
 
     def add_up(y, _):
         p0, p1 = recv_o[y, 0:8, :], recv_o[y, 8:16, :]
@@ -457,15 +525,9 @@
         for q in range(1, 4):
             end = jnp.where(row < 2 * q, end, lane_roll(tail, 64 - 32 * q))
         last = jnp.where(lane < 64, last, end)
-        c0, c1 = recv_c[y, 0:8, :], recv_c[y, 8:16, :]
-        turn = ROWS * odd
-        e0, e1 = pltpu.roll(c0, turn, 1), pltpu.roll(c1, turn, 1)
-        e2 = jnp.where(
-            head, pltpu.roll(c0, turn + 56, 1), pltpu.roll(c1, (turn + 112) % LANES, 1)
-        )
-        joined[y, 0:8, :] = p0 + jnp.where(keep, e0, 0.0)
-        joined[y, 8:16, :] = p1 + jnp.where(keep, e1, 0.0)
-        joined[y, 16:24, :] = last + jnp.where(keep, e2, 0.0)
+        joined[y, 0:8, :] = joined[y, 0:8, :] + p0
+        joined[y, 8:16, :] = joined[y, 8:16, :] + p1
+        joined[y, 16:24, :] = joined[y, 16:24, :] + last
         return _
 
     lax.fori_loop(0, NGY, add_up, 0, unroll=8)
@@ -506,6 +568,7 @@
 def local(scalar, velocity):
     vmem = pl.BlockSpec(memory_space=pltpu.VMEM)
     buffers = [
+        (3, LANES, 64),
         (208, LANES),
         (NGZ, 14, LANES),
         (NGZ, 4, LANES),
@@ -520,7 +583,7 @@
     ]
     later = [
         (192, 256),
-        (TILES, 96, LANES),
+        (TILES, PLANES, ROWS, LANES),
         (TILES, 192, LANES),
         (TILES, 96, LANES),
         (TILES, 24, LANES),
@@ -531,20 +594,20 @@
         (NX, LANES),
         (NX, LANES),
         (NGY, 18, LANES),
-        (NGY, 16, LANES),
+        (NGY, 14, LANES),
         (NGY, 18, LANES),
-        (NGY, 16, LANES),
+        (NGY, 14, LANES),
         (NGY, ROWS, LANES),
     ]
     return pl.pallas_call(
         kernel,
-        out_shape=jax.ShapeDtypeStruct((PLANES, ROWS, NX), F32),
-        in_specs=[vmem, vmem],
+        out_shape=pltpu.VMEM((PLANES, ROWS, NX), F32),
+        in_specs=[pl.BlockSpec(memory_space=pl.ANY)] * 2,
         out_specs=vmem,
         scratch_shapes=[pltpu.VMEM(s, F32) for s in buffers]
         + [pltpu.VMEM((256, NX), BF16)]
         + [pltpu.VMEM(s, F32) for s in later]
-        + [pltpu.SemaphoreType.DMA((16,))],
+        + [pltpu.SemaphoreType.DMA((20,))],
         compiler_params=pltpu.CompilerParams(collective_id=0, has_side_effects=True),
     )(scalar, velocity.transpose(0, 2, 3, 1).reshape(3, LANES, 64))
 

time: 53.1 us -> 49.1 us (0.925)
  Pallas kernels: 51.3 us -> 48.3 us
  local copies, waits for them, and re-layouts: 1.69 us -> 0.72 us
    pallas_call x1, Pallas kernels: 51.3 us -> 48.3 us  [local(): pl.pallas_call(kernel, out_shape=pltpu.VMEM((PLANES, ROWS, NX), F32), in_...]
    unnamed x1, local copies, waits for them, and re-layouts: 1.69 us -> 0.72 us
where the time goes in v3:
time: 49.1 us; the launch traced here: 49 us
  Pallas kernels  48.3 us (98%)
  local copies, waits for them, and re-layouts  0.72 us (1%)
    pallas_call x1, Pallas kernels, local(): pl.pallas_call(kernel, out_shape=pltpu.VMEM((PLANES, ROWS, NX), F32), in_...  48.3 us

profile of v3, /device:TPU:1, one launch (start us, length us, event | category | flops | bytes accessed | tf_op | source)
XLA Modules:
  0.0 49.0 jit_solution(11927525755556614788)
XLA Ops:
  0.0 48.3 %shard_map.28 = f32[4,24,768]{2,1,0:T(8,128)S(1)} custom-call(f32[4,24,768]{2,1,0:T(8,128)} %scalar_ref.1, f32[3,128,64]{2,1,0:T(8,128)} %bitcast.3), custom_call_target="tpu_custom_call" | custom-call | tf_op jit(solution)/shard_map/pallas_call | solution.py:602
  48.3 0.7 %copy.4 = f32[4,24,768]{2,1,0:T(8,128)} copy(f32[4,24,768]{2,1,0:T(8,128)S(1)} %shard_map.28) | data formatting | bytes 589824

commit v4 on v3

--- a/solution.py
+++ b/solution.py
@@ -36,24 +36,26 @@
 
 def products(q, d):
     a = jnp.abs(d)
-    b = 1.0 - a
-    w = a * b
-    p3 = (w * (a * a)) * (7.0 / 24.0 - (5.0 / 24.0) * a)
-    pm2 = w * (1.0 / 12.0 + a * (1.0 / 24.0 + a * (-1.0 / 3.0 + (5.0 / 24.0) * a)))
-    p2 = w * (-1.0 / 12.0 + a * (-1.0 / 8.0 + a * (-3.0 / 2.0 + (25.0 / 24.0) * a)))
-    pm1 = w * (-2.0 / 3.0 + (a * a) * (13.0 / 8.0 - (25.0 / 24.0) * a))
-    p1 = a + pm1 + 2.0 * (pm2 - p2) - 3.0 * p3
-    p0 = 1.0 - (p1 + pm1) - (p2 + pm2) - p3
-    right = d >= 0.0
-    q0, q1, qm1, q2, qm2, q3 = (q * p for p in (p0, p1, pm1, p2, pm2, p3))
+    d2 = d * d
+    d3 = d2 * d
+    s = (d3 - d) * (1.0 / 12.0)
+    half = 0.5 * d
+    r = s * half
+    odd3 = d3 * ((1.0 - a) * (7.0 / 48.0 - (5.0 / 48.0) * a))
+    even3 = jnp.abs(odd3)
+    even2 = r - 6.0 * even3
+    odd2 = s - 4.0 * odd3
+    even1 = (0.5 * d2 - 4.0 * r) + 15.0 * even3
+    odd1 = (half - 2.0 * s) + 5.0 * odd3
+    middle = 1.0 - 2.0 * ((even1 + even2) + even3)
     return {
-        0: q0,
-        1: jnp.where(right, q1, qm1),
-        -1: jnp.where(right, qm1, q1),
-        2: jnp.where(right, q2, qm2),
-        -2: jnp.where(right, qm2, q2),
-        3: jnp.where(right, q3, 0.0),
-        -3: jnp.where(right, 0.0, q3),
+        0: q * middle,
+        1: q * (even1 + odd1),
+        -1: q * (even1 - odd1),
+        2: q * (even2 + odd2),
+        -2: q * (even2 - odd2),
+        3: q * (even3 + odd3),
+        -3: q * (even3 - odd3),
     }
 
 
@@ -106,6 +108,7 @@
     recv_c,
     joined,
     sems,
+    column,
 ):
     gy, gz = lax.axis_index("gy"), lax.axis_index("gz")
     odd = gz % 2
@@ -113,7 +116,6 @@
     partner = gz + 1 - 2 * odd
     other = gz - 1 + 2 * odd
     has_other = jnp.logical_and(other >= 0, other < NGZ)
-    n_other = has_other.astype(jnp.int32)
     lane = lax.broadcasted_iota(jnp.int32, (8, LANES), 1)
 
     take_vel = pltpu.make_async_copy(vel_ref, vel, sems.at[16])
@@ -143,17 +145,9 @@
         greet((gy + i) % NGY, gz)
         return _
 
-    def greet_o(i, _):
-        greet((gy + i) % NGY, other)
-        return _
-
     lax.fori_loop(0, NGZ, greet_zn, 0)
     lax.fori_loop(1, NGZ, greet_z, 0)
     lax.fori_loop(2, NGY - 1, greet_y, 0)
-
-    @pl.when(has_other)
-    def _():
-        lax.fori_loop(2, NGY - 1, greet_o, 0)
 
     @pl.when(jnp.logical_not(has_other))
     def _():
@@ -210,7 +204,14 @@
                 hal_up[at, columns] = scal[t, z, k : k + 1, :]
                 hal_dn[at, columns] = scal[t, z, 21 + k : 22 + k, :]
 
-    pl.semaphore_wait(barrier, 105 - 29 + 29 * n_other)
+    pl.semaphore_wait(barrier, 76)
+
+    @pl.when(has_other)
+    def _():
+        pl.semaphore_signal(
+            column, inc=1, device_id={"gy": gy, "gz": other}, device_id_type=MESH
+        )
+
 
     def send_z(i, _):
         z = (gz + offset_of(i)) % NGZ
@@ -466,6 +467,10 @@
 
         return carry
 
+    @pl.when(has_other)
+    def _():
+        pl.semaphore_wait(column, 1)
+
     lax.fori_loop(0, 2, cross_step, 0)
 
     target = pl.ds(pl.multiple_of(ROWS * (1 - odd), 8), 72)
@@ -516,7 +521,7 @@
 
     wait_for(recv_o.at[0 : NGY - 1], sems.at[15])
 
-    def add_up(y, _):
+    def last_rows(y):
         p0, p1 = recv_o[y, 0:8, :], recv_o[y, 8:16, :]
         tail = recv_o[y, 16:18, :]
         tail = jnp.concatenate([tail, tail, tail, tail], axis=0)
@@ -524,33 +529,28 @@
         end = lane_roll(tail, 64)
         for q in range(1, 4):
             end = jnp.where(row < 2 * q, end, lane_roll(tail, 64 - 32 * q))
-        last = jnp.where(lane < 64, last, end)
-        joined[y, 0:8, :] = joined[y, 0:8, :] + p0
-        joined[y, 8:16, :] = joined[y, 8:16, :] + p1
-        joined[y, 16:24, :] = joined[y, 16:24, :] + last
-        return _
-
-    lax.fori_loop(0, NGY, add_up, 0, unroll=8)
-
-    def place(x, _):
-        rows = pl.ds(pl.multiple_of(8 * x, 8), 8)
+        return jnp.where(lane < 64, last, end)
+
+    for y in range(NGY):
+        joined[y, 16:24, :] = joined[y, 16:24, :] + last_rows(y)
+    for x in range(3):
+        rows = slice(8 * x, 8 * x + 8)
         for t in range(TILES):
             pieces = [None] * PLANES
             for y in range(LANES * t // ROWS, (LANES * t + LANES - 1) // ROWS + 1):
                 value = joined[y, rows, :]
+                if x < 2:
+                    value = value + recv_o[y, rows, :]
                 edge_at = ROWS * y - LANES * t
                 for z in range(PLANES):
-                    turned = lane_roll(value, ROWS * (y - z))
+                    turned_to = lane_roll(value, ROWS * (y - z))
                     pieces[z] = (
-                        turned
+                        turned_to
                         if pieces[z] is None
-                        else jnp.where(lane < edge_at, pieces[z], turned)
+                        else jnp.where(lane < edge_at, pieces[z], turned_to)
                     )
             for z in range(PLANES):
                 out_ref[z, rows, LANES * t : LANES * t + LANES] = pieces[z]
-        return _
-
-    lax.fori_loop(0, 3, place, 0)
 
     wait_for(send_v.at[0:15], sems.at[0])
     wait_for(send_n, sems.at[2])
@@ -607,7 +607,7 @@
         scratch_shapes=[pltpu.VMEM(s, F32) for s in buffers]
         + [pltpu.VMEM((256, NX), BF16)]
         + [pltpu.VMEM(s, F32) for s in later]
-        + [pltpu.SemaphoreType.DMA((20,))],
+        + [pltpu.SemaphoreType.DMA((20,)), pltpu.SemaphoreType.REGULAR],
         compiler_params=pltpu.CompilerParams(collective_id=0, has_side_effects=True),
     )(scalar, velocity.transpose(0, 2, 3, 1).reshape(3, LANES, 64))
 

time: 49.1 us -> 45.6 us (0.929)
  Pallas kernels: 48.3 us -> 44.7 us
    pallas_call x1, Pallas kernels: 48.3 us -> 44.7 us  [local(): pl.pallas_call(kernel, out_shape=pltpu.VMEM((PLANES, ROWS, NX), F32), in_...]
where the time goes in v4:
time: 45.6 us; the launch traced here: 45.4 us
  Pallas kernels  44.7 us (98%)
  local copies, waits for them, and re-layouts  0.72 us (2%)
    pallas_call x1, Pallas kernels, local(): pl.pallas_call(kernel, out_shape=pltpu.VMEM((PLANES, ROWS, NX), F32), in_...  44.7 us

profile of v4, /device:TPU:1, one launch (start us, length us, event | category | flops | bytes accessed | tf_op | source)
XLA Modules:
  0.0 45.4 jit_solution(9968591353606728487)
XLA Ops:
  0.0 44.7 %shard_map.28 = f32[4,24,768]{2,1,0:T(8,128)S(1)} custom-call(f32[4,24,768]{2,1,0:T(8,128)} %scalar_ref.1, f32[3,128,64]{2,1,0:T(8,128)} %bitcast.3), custom_call_target="tpu_custom_call" | custom-call | tf_op jit(solution)/shard_map/pallas_call | solution.py:602
  44.7 0.7 %copy.4 = f32[4,24,768]{2,1,0:T(8,128)} copy(f32[4,24,768]{2,1,0:T(8,128)S(1)} %shard_map.28) | data formatting | bytes 589824

commit v5 on v4

--- a/solution.py
+++ b/solution.py
@@ -69,6 +69,25 @@
     return value if amount == 0 else pltpu.roll(value, amount, 0)
 
 
+def exchanged(values, width, lane):
+    values = list(values)
+    step = len(values) // 2
+    while step:
+        stay = jnp.zeros(lane.shape, jnp.bool_)
+        for c in range(len(values)):
+            if not c & step:
+                stay = jnp.logical_or(
+                    stay, jnp.logical_and(lane >= width * c, lane < width * (c + 1))
+                )
+        for i in range(len(values)):
+            if not i & step:
+                a, b = values[i], values[i + step]
+                values[i] = jnp.where(stay, a, lane_roll(b, width * step))
+                values[i + step] = jnp.where(stay, lane_roll(a, -width * step), b)
+        step //= 2
+    return values
+
+
 def offset_of(i):
     half = (i + 1) // 2
     return half * (2 * (i % 2) - 1) + NGY
@@ -96,6 +115,7 @@
     fine,
     field,
     edge,
+    shift,
     own,
     cross,
     part,
@@ -236,37 +256,30 @@
     wait_for(recv_n, sems.at[3])
     wait_for(recv_p, sems.at[5])
 
+    for half in range(2):
+        columns = pl.ds(LANES * half, LANES)
+        for first, count in ((0, 8), (8, 6)):
+            tiles = exchanged(
+                [recv_v[8 * half + i, first : first + count, :] for i in range(8)],
+                16,
+                lane[0:count],
+            )
+            for c in range(8):
+                base = 16 * (c + 2) + first
+                coarse[base : base + count, columns] = tiles[c]
     for c in range(8):
-        for half in range(2):
-            top = jnp.zeros((8, LANES), F32)
-            low = jnp.zeros((6, LANES), F32)
-            for i in range(8):
-                g = 8 * half + i
-                here = jnp.logical_and(lane >= 16 * i, lane < 16 * i + 16)
-                top = jnp.where(here, lane_roll(recv_v[g, 0:8, :], 16 * (i - c)), top)
-                low = jnp.where(
-                    here[0:6], lane_roll(recv_v[g, 8:14, :], 16 * (i - c)), low
-                )
-            base = 16 * (c + 2)
-            columns = pl.ds(LANES * half, LANES)
-            coarse[base : base + 8, columns] = top
-            coarse[base + 8 : base + 14, columns] = low
-            coarse[base + 14 : base + 16, columns] = jnp.zeros((2, LANES), F32)
-    for c in (-2, -1, 8, 9):
-        source, offset, chunks = (recv_n, c - 8, 4) if c > 0 else (recv_p, c + 2, 2)
-        base = 16 * (c + 2)
-        for half in range(2):
-            columns = pl.ds(LANES * half, LANES)
-            for q in range(4):
-                total = jnp.zeros((4, LANES), F32)
-                if q < chunks:
-                    for i in range(8):
-                        here = jnp.logical_and(lane4 >= 16 * i, lane4 < 16 * i + 16)
-                        rows = source[8 * half + i]
-                        total = jnp.where(
-                            here, lane_roll(rows, 16 * i - 32 * q - 16 * offset), total
-                        )
-                coarse[base + 4 * q : base + 4 * q + 4, columns] = total
+        base = 16 * (c + 2) + 14
+        coarse[base : base + 2, :] = jnp.zeros((2, 2 * LANES), F32)
+    for source, first in ((recv_p, -2), (recv_n, 8)):
+        tiles = exchanged(
+            [jnp.concatenate([source[i], source[8 + i]], axis=0) for i in range(8)],
+            16,
+            lane,
+        )
+        for e in range(8):
+            base = 16 * (first + e % 2 + 2) + 4 * (e // 2)
+            coarse[base : base + 4, 0:LANES] = tiles[e][0:4]
+            coarse[base : base + 4, LANES : 2 * LANES] = tiles[e][4:8]
     value = coarse[...]
     high = value.astype(BF16)
     low = (value - high.astype(F32)).astype(BF16)
@@ -301,35 +314,50 @@
     def mixed(base, following, k):
         return base if k == 0 else base * (1.0 - k / 3.0) + following * (k / 3.0)
 
-    def sweep_x(q, u):
-        d = moved_by(u, lane_roll(u, 1), lane_roll(u, -1))
-        terms = products(q, d)
+    def shift_rows(group, k):
+        return pl.ds(pl.multiple_of(ROWS * group + 8 * k, 8), 8)
+
+    def shifts(group, base, following):
+        for k in range(3):
+            u = mixed(base, following, k)
+            d = moved_by(u, lane_roll(u, 1), lane_roll(u, -1))
+            spread(shift, shift_rows(group, k), d)
+
+    def plane_shifts(z):
+        shifts(z, whole(functools.partial(level, 0, z)), whole(functools.partial(level, 1, z)))
+
+    def sweep_x(q, group, k, ref, rows):
+        terms = products(q, whole(lambda t: shift[t, shift_rows(group, k), :]))
         total = terms[0]
         for m in (-3, -2, -1, 1, 2, 3):
             total = total + lane_roll(terms[m], m)
-        return total
-
-    def plane_x(z, _):
-        base = whole(functools.partial(level, 0, z))
-        following = whole(functools.partial(level, 1, z))
+        spread(ref, rows, total)
+
+    def plane_x(z):
         for k in range(3):
             q = whole(lambda t: scal[t, z, pl.ds(k, 8, stride=3), :])
-            rows = pl.ds(pl.multiple_of(24 * z + 8 * k, 8), 8)
-            spread(field, rows, sweep_x(q, mixed(base, following, k)))
-        return _
-
-    lax.fori_loop(0, PLANES, plane_x, 0)
+            sweep_x(q, z, k, field, shift_rows(z, k))
+
+    def step_x(z, _):
+        plane_shifts(z + 1)
+        plane_x(z)
+        return _
+
+    plane_shifts(0)
+    lax.fori_loop(0, PLANES - 1, step_x, 0)
+    shifts(
+        PLANES,
+        whole(functools.partial(edge_level, 0, 0)),
+        whole(functools.partial(edge_level, 1, 0)),
+    )
+    plane_x(PLANES - 1)
     wait_for(got_up, sems.at[7])
     wait_for(got_dn, sems.at[9])
-    base = whole(functools.partial(edge_level, 0, 0))
-    following = whole(functools.partial(edge_level, 1, 0))
     for k in range(3):
         q = jnp.concatenate(
             [got_up[4 * k : 4 * k + 4, :], got_dn[4 * k : 4 * k + 4, :]], axis=0
         )
-        spread(
-            edge, slice(8 * k, 8 * k + 8), sweep_x(q, mixed(base, following, k))
-        )
+        sweep_x(q, PLANES, k, edge, slice(8 * k, 8 * k + 8))
 
     row = lax.broadcasted_iota(jnp.int32, (8, LANES), 0)
 
@@ -431,13 +459,12 @@
 
     def pack_own(y):
         v = rows_of(t_own, y)
-        send_o[y, 0:8, :] = jnp.where(lane < 96, v[0], lane_roll(v[2], 96))
-        send_o[y, 8:16, :] = jnp.where(lane < 96, v[1], lane_roll(v[2], 64))
-        tail = lane_roll(v[2], 64)
-        for q in range(1, 4):
-            piece = row_roll(lane_roll(v[2], 32 * q + 64), -2 * q)
-            tail = jnp.where(lane < 32 * q, tail, piece)
-        send_o[y, 16:18, :] = tail[0:2]
+        end = lane_roll(v[2], 32)
+        first = jnp.where(row >= 2, lane_roll(v[2], 96), row_roll(end, -2))
+        second = jnp.where(row >= 2, lane_roll(v[2], 64), row_roll(end, -4))
+        send_o[y, 0:8, :] = jnp.where(lane < 96, v[0], first)
+        send_o[y, 8:16, :] = jnp.where(lane < 96, v[1], second)
+        send_o[y, 16:18, :] = jnp.where(lane < 96, v[2], row_roll(end, -6))[0:2]
 
     def send_own(y):
         @pl.when(y != gy)
@@ -525,11 +552,11 @@
         p0, p1 = recv_o[y, 0:8, :], recv_o[y, 8:16, :]
         tail = recv_o[y, 16:18, :]
         tail = jnp.concatenate([tail, tail, tail, tail], axis=0)
-        last = jnp.where(lane < 32, lane_roll(p0, 32), lane_roll(p1, 64))
-        end = lane_roll(tail, 64)
-        for q in range(1, 4):
-            end = jnp.where(row < 2 * q, end, lane_roll(tail, 64 - 32 * q))
-        return jnp.where(lane < 64, last, end)
+        end = jnp.where(row < 6, row_roll(p1, 4), tail)
+        end = lane_roll(jnp.where(row < 4, row_roll(p0, 2), end), 96)
+        last = jnp.where(lane < 64, lane_roll(p1, 64), end)
+        last = jnp.where(lane < 32, lane_roll(p0, 32), last)
+        return jnp.where(row < 2, tail, last)
 
     for y in range(NGY):
         joined[y, 16:24, :] = joined[y, 16:24, :] + last_rows(y)
@@ -587,6 +614,7 @@
         (TILES, 192, LANES),
         (TILES, 96, LANES),
         (TILES, 24, LANES),
+        (TILES, 120, LANES),
         (TILES, LANES, LANES),
         (TILES, LANES, LANES),
         (TILES, 72, LANES),

time: 45.6 us -> 45.1 us (0.989)
  Pallas kernels: 44.7 us -> 44.2 us
    pallas_call x1, Pallas kernels: 44.7 us -> 44.2 us  [local(): pl.pallas_call(kernel, out_shape=pltpu.VMEM((PLANES, ROWS, NX), F32), in_...]
where the time goes in v5:
time: 45.1 us; the launch traced here: 44.9 us
  Pallas kernels  44.2 us (98%)
  local copies, waits for them, and re-layouts  0.72 us (2%)
    pallas_call x1, Pallas kernels, local(): pl.pallas_call(kernel, out_shape=pltpu.VMEM((PLANES, ROWS, NX), F32), in_...  44.2 us

profile of v5, /device:TPU:1, one launch (start us, length us, event | category | flops | bytes accessed | tf_op | source)
XLA Modules:
  0.0 44.9 jit_solution(7695272750141508303)
XLA Ops:
  0.0 44.2 %shard_map.28 = f32[4,24,768]{2,1,0:T(8,128)S(1)} custom-call(f32[4,24,768]{2,1,0:T(8,128)} %scalar_ref.1, f32[3,128,64]{2,1,0:T(8,128)} %bitcast.3), custom_call_target="tpu_custom_call" | custom-call | tf_op jit(solution)/shard_map/pallas_call | solution.py:630
  44.2 0.7 %copy.4 = f32[4,24,768]{2,1,0:T(8,128)} copy(f32[4,24,768]{2,1,0:T(8,128)S(1)} %shard_map.28) | data formatting | bytes 589824

commit v6 on v5

--- a/solution.py
+++ b/solution.py
@@ -477,7 +477,7 @@
         return ref.at[pl.ds(TILES // 2 * h, TILES // 2)]
 
     def cross_step(step, carry):
-        h = (gy + step) % 2
+        h = (gy // 4 + step) % 2
 
         def tiles(i, _):
             return tile_step(TILES // 2 * h + i, _)
@@ -503,7 +503,7 @@
     target = pl.ds(pl.multiple_of(ROWS * (1 - odd), 8), 72)
 
     def own_step(step, _):
-        h = (gy + step) % 2
+        h = (gy // 4 + step) % 2
         wait_for(half_of(recv_d, h), sems.at[18 + step])
         tiles = pl.ds(TILES // 2 * h, TILES // 2)
         own[tiles, target, :] = own[tiles, target, :] + recv_d[tiles]

time: 45.1 us -> 45.1 us (level)
  no operation moved by 1% of the time
where the time goes in v6:
time: 45.1 us; the launch traced here: 45 us
  Pallas kernels  44.3 us (98%)
  local copies, waits for them, and re-layouts  0.72 us (2%)
    pallas_call x1, Pallas kernels, local(): pl.pallas_call(kernel, out_shape=pltpu.VMEM((PLANES, ROWS, NX), F32), in_...  44.3 us

profile of v6, /device:TPU:1, one launch (start us, length us, event | category | flops | bytes accessed | tf_op | source)
XLA Modules:
  0.0 45.0 jit_solution(10495328522320104803)
XLA Ops:
  0.0 44.3 %shard_map.28 = f32[4,24,768]{2,1,0:T(8,128)S(1)} custom-call(f32[4,24,768]{2,1,0:T(8,128)} %scalar_ref.1, f32[3,128,64]{2,1,0:T(8,128)} %bitcast.3), custom_call_target="tpu_custom_call" | custom-call | tf_op jit(solution)/shard_map/pallas_call | solution.py:630
  44.3 0.7 %copy.4 = f32[4,24,768]{2,1,0:T(8,128)} copy(f32[4,24,768]{2,1,0:T(8,128)S(1)} %shard_map.28) | data formatting | bytes 589824
